TPU v7x, 32 devices: a whole 2x2x4 slice. The times are simulated.
32 devices in a mesh: blk: 8 (over z, x), rows: 4 (over y, core).
Axes of the slice: x: 2, y: 2, z: 4, core: 2. Of those that a mesh axis runs over, the one named last changes fastest.
Arguments:
- columns: float32 [512, 16384], P('blk', 'rows'), may hold values from -100 to 100
- plan: int32 [3, 16], replicated, may hold values from 0 to 15, as said below
Outputs:
- swept: float32 [512, 16384], P('blk', 'rows')
- off_ratio: float32 [3], replicated
Inputs may be any that keep to these rules, and one draw needn't show every extreme that they name: `plan`: row s is a permutation of the 16 positions (position k is slot k % 2 of blk index k // 2). In each row there are a slot t and a number m of 1 to 7 such that the block in slot t of every blk index i goes to slot t of blk index (i + m) modulo 16 / 2, and every other block stays where it is.
All inputs are finite; a program needn't handle non-finite values. Where the computation divides by a largest or mean magnitude, that divisor is 1e-20 or more.
Results may differ from a plain program's by a relative error of at most 0.00011.
Values sent between devices are 32-bit elements; how exact they have to be, the bound alone decides.
No kernel may reach another device: no remote copies, remote signals or barrier semaphores. Data moves between devices by JAX's collectives and lax.ppermute only.
A program may use at most 64 MiB of HBM per device.

v0:
```python
from functools import partial
import jax
import jax.numpy as jnp
from jax import lax
from jax.sharding import PartitionSpec as P

STEPS = 3
EIG_ITERS = 3
NS_ITERS = 8
PRECISE = lax.Precision.HIGHEST


def shifted(value, axis, steps):
    count = lax.axis_size(axis)
    pairs = [(source, (source + steps) % count) for source in range(count)]
    return lax.ppermute(value, axis, pairs)


def matmul(left, right):
    return jnp.matmul(left, right, precision=PRECISE, preferred_element_type=jnp.float32)


def orthonormal(matrix):
    lengths = jnp.sqrt(jnp.sum(matrix * matrix, axis=0, keepdims=True))
    normed = matrix / lengths
    inner = matmul(normed.T, normed)
    bound = jnp.max(jnp.sum(jnp.abs(inner), axis=1))
    normed = normed / jnp.sqrt(bound)
    for turn_index in range(NS_ITERS):
        normed = 1.5 * normed - 0.5 * matmul(normed, matmul(normed.T, normed))
    return normed


def pair_rotation(gram_sum):
    rotation = jnp.eye(gram_sum.shape[0], dtype=gram_sum.dtype)
    for turn_index in range(EIG_ITERS):
        rotation = orthonormal(matmul(gram_sum, rotation))
    return rotation


def move_by(values, distance):
    return shifted(values, "blk", distance)


def local(columns, plan):
    block_width = columns.shape[0] // 2
    cycle_size = lax.axis_size("blk")
    eye_mask = jnp.eye(2 * block_width, dtype=bool)
    current = columns
    off_list = []
    diag_list = []
    for step_index in range(STEPS):
        partial_gram = matmul(current, current.T)
        gram_sum = lax.psum(partial_gram, "rows")
        off_part = jnp.where(eye_mask, 0.0, gram_sum)
        diag_part = jnp.where(eye_mask, gram_sum, 0.0)
        off_local = jnp.sum(off_part * off_part)
        diag_local = jnp.sum(diag_part * diag_part)
        off_total, diag_total = lax.psum((off_local, diag_local), "blk")
        off_list.append(off_total)
        diag_list.append(diag_total)
        rotation = pair_rotation(gram_sum)
        rotated = matmul(rotation.T, current)
        first_dest = plan[step_index, 0]
        second_dest = plan[step_index, 1]
        partner_step = jnp.maximum(first_dest // 2, second_dest // 2)
        leaving_high = second_dest != 1
        moving = jnp.where(leaving_high, rotated[block_width:], rotated[:block_width])
        staying = jnp.where(leaving_high, rotated[:block_width], rotated[block_width:])
        branches = [partial(move_by, distance=distance) for distance in range(1, cycle_size)]
        moving = lax.switch(partner_step - 1, branches, moving)
        current = jnp.where(
            leaving_high,
            jnp.concatenate([staying, moving], axis=0),
            jnp.concatenate([moving, staying], axis=0),
        )
    off_sums = jnp.stack(off_list)
    diag_sums = jnp.stack(diag_list)
    return (current, jnp.sqrt(off_sums) / jnp.sqrt(diag_sums))


def solution(mesh):
    return jax.shard_map(
        local,
        mesh=mesh,
        in_specs=(P("blk", "rows"), P()),
        out_specs=(P("blk", "rows"), P()),
        check_vma=False,
    )
```

profile of v0, /device:TPU:0, one launch (start us, length us, event | category | flops | bytes accessed | tf_op | source)
XLA Modules:
  0.0 189.1 jit_solution(8808458993383925959)
XLA Ops:
  0.6 1.6 fusion.124
  19.2 1.0 fusion.125
  20.2 12.9 %psum.63 = f32[64,64]{1,0:T(8,128)S(1)} all-reduce(f32[64,64]{1,0:T(8,128)S(1)} %fusion.125), channel_id=1, replica_groups=mesh['blk'=8,'rows'=4] {'rows'}, use_global_device_ids=true, to_apply=%region_0.0 | all-reduce | flops 4096 | bytes 32768 | tf_op jit(solution)/shard_map/psum | solution.py:54
  33.1 0.7 multiply_reduce_fusion.2
  49.1 1.0 fusion.147
  50.2 13.9 %conditional.3 = (f32[32,4096]{1,0:T(8,128)}) conditional(s32[]{:T(128)} %clamp.9, f32[32,4096]{1,0:T(8,128)S(1)} %get-tuple-element.64, f32[32,4096]{1,0:T(8,128)S(1)} %get-tuple-element.64, f32[32,4096]{1,0:T(8,128)S(1)} %get-tuple-element.64, f32[32,4096]{1,0:T(8,128)S(1)} %get-tuple-element.64, ...), branch_computations={%region_10.11_spmd, %region_11.12_spmd, %region_12.13_spmd, %regio... | conditional | bytes 2097200 | solution.py:71
  50.2 3.7 %collective-permute-start.5 = (f32[32,4096]{1,0:T(8,128)S(1)}, f32[32,4096]{1,0:T(8,128)}, u32[]{:S(2)}, u32[]{:S(2)}) collective-permute-start(f32[32,4096]{1,0:T(8,128)S(1)} %param.5), channel_id=1, source_target_pairs={{0,24},{4,28},{8,0},{12,4},{16,8},{20,12},{24,16},{28,20},{1,25},{... | collective-permute-start | bytes 1572872 | tf_op jit(solution)/shard_map/cond/branch_5_fun/ppermute | solution.py:16
  53.9 10.2 %collective-permute-done.5 = f32[32,4096]{1,0:T(8,128)} collective-permute-done((f32[32,4096]{1,0:T(8,128)S(1)}, f32[32,4096]{1,0:T(8,128)}, u32[]{:S(2)}, u32[]{:S(2)}) %collective-permute-start.5) | collective-permute-done | bytes 524320 | tf_op jit(solution)/shard_map/cond/branch_5_fun/ppermute | solution.py:16
  64.0 2.7 %fusion.84 = f32[64,64]{1,0:T(8,128)S(1)} fusion(f32[32,4096]{1,0:T(8,128)} %get-tuple-element.89, f32[32,4096]{1,0:T(8,128)S(1)} %get-tuple-element.63, pred[]{:T(512)S(6)} %ne.49), kind=kOutput, calls=%fused_computation.168 | convolution fusion | flops 202113024 | bytes 1064961 | tf_op jit(solution)/shard_map/dot_general | solution.py:20
  66.8 10.7 %psum.64 = f32[64,64]{1,0:T(8,128)S(1)} all-reduce(f32[64,64]{1,0:T(8,128)S(1)} %fusion.84), channel_id=1, replica_groups=mesh['blk'=8,'rows'=4] {'rows'}, use_global_device_ids=true, to_apply=%region_17.18 | all-reduce | flops 4096 | bytes 32768 | tf_op jit(solution)/shard_map/psum | solution.py:54
  77.5 0.7 multiply_reduce_fusion.1
  93.4 2.3 %fusion.83 = f32[64,4096]{1,0:T(8,128)S(1)} fusion(f32[64,64]{1,0:T(8,128)S(1)} %fusion.24, f32[32,4096]{1,0:T(8,128)} %get-tuple-element.89, f32[32,4096]{1,0:T(8,128)S(1)} %get-tuple-element.63, pred[]{:T(512)S(6)} %ne.49), kind=kOutput, calls=%fused_computation.167 | convolution fusion | flops 202113024 | bytes 2113537 | tf_op jit(solution)/shard_map/dot_general | solution.py:20
  95.8 27.1 %conditional.4 = (f32[32,4096]{1,0:T(8,128)}) conditional(s32[]{:T(128)} %clamp.10, f32[32,4096]{1,0:T(8,128)S(1)} %get-tuple-element.62, f32[32,4096]{1,0:T(8,128)S(1)} %get-tuple-element.62, f32[32,4096]{1,0:T(8,128)S(1)} %get-tuple-element.62, f32[32,4096]{1,0:T(8,128)S(1)} %get-tuple-element.62, ...), branch_computations={%region_27.28_spmd, %region_28.29_spmd, %region_29.30_spmd, %regio... | conditional | bytes 2097200 | solution.py:71
  95.8 1.5 collective-permute-start.9
  97.4 25.6 %collective-permute-done.9 = f32[32,4096]{1,0:T(8,128)} collective-permute-done((f32[32,4096]{1,0:T(8,128)S(1)}, f32[32,4096]{1,0:T(8,128)}, u32[]{:S(2)}, u32[]{:S(2)}) %collective-permute-start.9) | collective-permute-done | bytes 524320 | tf_op jit(solution)/shard_map/cond/branch_2_fun/ppermute | solution.py:16
  122.9 2.7 %fusion.82 = f32[64,64]{1,0:T(8,128)S(1)} fusion(f32[32,4096]{1,0:T(8,128)} %get-tuple-element.90, f32[32,4096]{1,0:T(8,128)S(1)} %get-tuple-element.61, pred[]{:T(512)S(6)} %ne.48), kind=kOutput, calls=%fused_computation.166 | convolution fusion | flops 202113024 | bytes 1064961 | tf_op jit(solution)/shard_map/dot_general | solution.py:20
  125.7 10.3 %psum.65 = f32[64,64]{1,0:T(8,128)S(1)} all-reduce(f32[64,64]{1,0:T(8,128)S(1)} %fusion.82), channel_id=1, replica_groups=mesh['blk'=8,'rows'=4] {'rows'}, use_global_device_ids=true, to_apply=%region_34.35 | all-reduce | flops 4096 | bytes 32768 | tf_op jit(solution)/shard_map/psum | solution.py:54
  136.6 18.0 %all-reduce = (f32[1]{0:T(128)}, f32[1]{0:T(128)}, f32[1]{0:T(128)}, f32[1]{0:T(128)}, f32[1]{0:T(128)}, /*index=5*/f32[1]{0:T(128)}) all-reduce(f32[1]{0:T(128)} %bitcast.8, f32[1]{0:T(128)} %bitcast.7, f32[1]{0:T(128)} %bitcast.6, f32[1]{0:T(128)} %bitcast.11, f32[1]{0:T(128)} %bitcast.10, ...), channel_id=1, replica_groups=mesh['blk'=8,'rows'=4] {'blk'}, use_global_device_ids=true, to_apply=%region_56.57 | all-reduce | flops 6 | bytes 48 | tf_op jit(solution)/shard_map/psum | solution.py:59
  154.6 4.3 %fusion.119 = f32[3]{0:T(128)} fusion(f32[1]{0:T(128)} %get-tuple-element.53, f32[1]{0:T(128)} %get-tuple-element.54, f32[1]{0:T(128)} %get-tuple-element.55, f32[1]{0:T(128)} %get-tuple-element.56, f32[1]{0:T(128)} %get-tuple-element.57, f32[1]{0:T(128)} %get-tuple-element.58), kind=kLoop, calls=%fused_computation.235 | loop fusion | flops 15 | bytes 36 | tf_op jit(solution)/shard_map/div | solution.py:79
  174.2 2.3 %fusion.81 = f32[64,4096]{1,0:T(8,128)S(1)} fusion(f32[64,64]{1,0:T(8,128)S(1)} %fusion, f32[32,4096]{1,0:T(8,128)} %get-tuple-element.90, f32[32,4096]{1,0:T(8,128)S(1)} %get-tuple-element.61, pred[]{:T(512)S(6)} %ne.48), kind=kOutput, calls=%fused_computation.165 | convolution fusion | flops 202113024 | bytes 2113537 | tf_op jit(solution)/shard_map/dot_general | solution.py:20
  176.6 10.3 %conditional.5 = (f32[32,4096]{1,0:T(8,128)}) conditional(s32[]{:T(128)} %clamp.11, f32[32,4096]{1,0:T(8,128)S(1)} %get-tuple-element.60, f32[32,4096]{1,0:T(8,128)S(1)} %get-tuple-element.60, f32[32,4096]{1,0:T(8,128)S(1)} %get-tuple-element.60, f32[32,4096]{1,0:T(8,128)S(1)} %get-tuple-element.60, ...), branch_computations={%region_44.45_spmd, %region_45.46_spmd, %region_46.47_spmd, %regio... | conditional | bytes 2097200 | solution.py:71
  176.6 2.1 %collective-permute-start.20 = (f32[32,4096]{1,0:T(8,128)S(1)}, f32[32,4096]{1,0:T(8,128)}, u32[]{:S(2)}, u32[]{:S(2)}) collective-permute-start(f32[32,4096]{1,0:T(8,128)S(1)} %param.20), channel_id=1, source_target_pairs={{0,28},{4,0},{8,4},{12,8},{16,12},{20,16},{24,20},{28,24},{1,29},{... | collective-permute-start | bytes 1572872 | tf_op jit(solution)/shard_map/cond/branch_6_fun/ppermute | solution.py:16
  178.7 8.2 %collective-permute-done.20 = f32[32,4096]{1,0:T(8,128)} collective-permute-done((f32[32,4096]{1,0:T(8,128)S(1)}, f32[32,4096]{1,0:T(8,128)}, u32[]{:S(2)}, u32[]{:S(2)}) %collective-permute-start.20) | collective-permute-done | bytes 524320 | tf_op jit(solution)/shard_map/cond/branch_6_fun/ppermute | solution.py:16
  186.8 2.3 %maximum_select_fusion.2 = f32[64,4096]{1,0:T(8,128)} fusion(f32[32,4096]{1,0:T(8,128)} %get-tuple-element.91, f32[32,4096]{1,0:T(8,128)S(1)} %get-tuple-element.59, pred[]{:T(512)S(6)} %ne.47), kind=kLoop, calls=%fused_computation.164 | loop fusion | flops 786432 | bytes 2097153 | tf_op jit(solution)/shard_map/jit(_where)/select_n | solution.py:72
  (195 shorter events, 39.1 us)
Async XLA Ops:
  0.6 18.6 %copy-start = (f32[64,4096]{1,0:T(8,128)S(1)}, f32[64,4096]{1,0:T(8,128)}, u32[]{:S(2)}) copy-start(f32[64,4096]{1,0:T(8,128)} %param.23) | copy-start | bytes 3145732
  50.2 13.8 %collective-permute-start.5 = (f32[32,4096]{1,0:T(8,128)S(1)}, f32[32,4096]{1,0:T(8,128)}, u32[]{:S(2)}, u32[]{:S(2)}) collective-permute-start(f32[32,4096]{1,0:T(8,128)S(1)} %param.5), channel_id=1, source_target_pairs={{0,24},{4,28},{8,0},{12,4},{16,8},{20,12},{24,16},{28,20},{1,25},{... | collective-permute-start | bytes 1572872 | tf_op jit(solution)/shard_map/cond/branch_5_fun/ppermute | solution.py:16
  95.8 27.1 %collective-permute-start.9 = (f32[32,4096]{1,0:T(8,128)S(1)}, f32[32,4096]{1,0:T(8,128)}, u32[]{:S(2)}, u32[]{:S(2)}) collective-permute-start(f32[32,4096]{1,0:T(8,128)S(1)} %param.9), channel_id=1, source_target_pairs={{0,12},{4,16},{8,20},{12,24},{16,28},{20,0},{24,4},{28,8},{1,13},{... | collective-permute-start | bytes 1572872 | tf_op jit(solution)/shard_map/cond/branch_2_fun/ppermute | solution.py:16
  176.6 10.2 %collective-permute-start.20 = (f32[32,4096]{1,0:T(8,128)S(1)}, f32[32,4096]{1,0:T(8,128)}, u32[]{:S(2)}, u32[]{:S(2)}) collective-permute-start(f32[32,4096]{1,0:T(8,128)S(1)} %param.20), channel_id=1, source_target_pairs={{0,28},{4,0},{8,4},{12,8},{16,12},{20,16},{24,20},{28,24},{1,29},{... | collective-permute-start | bytes 1572872 | tf_op jit(solution)/shard_map/cond/branch_6_fun/ppermute | solution.py:16
where the time goes:
time: 190 us; the launch traced here: 189 us
  blocking collectives  51.9 us (27%)
  matrix products  44.7 us (24%)
  waiting for transfers between devices  43.9 us (23%)
  between operations  25.2 us (13%)
  other arithmetic  14.3 us (8%)
  starting transfers between devices  7.26 us (4%)
    dot_general x168, matrix products, matmul(): jnp.matmul(left, right, precision=PRECISE, preferred_element_type=jnp.flo...  44.7 us
    ppermute x3, waiting for transfers between devices, shifted(): return lax.ppermute(value, axis, pairs)  43.9 us
    psum x3, blocking collectives, local(): gram_sum = lax.psum(partial_gram, 'rows')  33.9 us
    psum x1, blocking collectives, local(): off_total, diag_total = lax.psum((off_local, diag_local), 'blk')  18 us
    ppermute x3, starting transfers between devices, shifted(): return lax.ppermute(value, axis, pairs)  7.26 us
    reduce_max x9, other arithmetic, orthonormal(): bound = jnp.max(jnp.sum(jnp.abs(inner), axis=1))  5.47 us
    div x1, other arithmetic, local(): return (current, jnp.sqrt(off_sums) / jnp.sqrt(diag_sums))  4.33 us
  transfers between devices with their start and end apart: 3, of which 3 were waited for; matrix products, arithmetic and copies ran while one was open for 0% of the time, Pallas kernels for 0%

commit v1 on v0

--- a/solution.py
+++ b/solution.py
@@ -51,7 +51,10 @@
     diag_list = []
     for step_index in range(STEPS):
         partial_gram = matmul(current, current.T)
-        gram_sum = lax.psum(partial_gram, "rows")
+        update_surface = lambda axis_name, work_x: jnp.sum(
+            lax.all_gather(work_x, axis_name=axis_name), axis=0
+        )
+        gram_sum = update_surface("rows", partial_gram)
         off_part = jnp.where(eye_mask, 0.0, gram_sum)
         diag_part = jnp.where(eye_mask, gram_sum, 0.0)
         off_local = jnp.sum(off_part * off_part)

time: 190 us -> 176 us (0.926)
  blocking collectives: 51.9 us -> 35.6 us
  waiting for transfers between devices: 43.9 us -> 46.3 us
    psum x3 -> x0, blocking collectives: 33.9 us -> none  [local(): gram_sum = lax.psum(partial_gram, 'rows')]
    all_gather x0 -> x3, blocking collectives: none -> 17.6 us  [local(): lax.all_gather(work_x, axis_name=axis_name)]
    ppermute x3, waiting for transfers between devices: 43.9 us -> 46.3 us  [shifted(): return lax.ppermute(value, axis, pairs)]
where the time goes in v1:
time: 176 us; the launch traced here: 175 us
  waiting for transfers between devices  46.3 us (26%)
  matrix products  44.7 us (25%)
  blocking collectives  35.6 us (20%)
  between operations  25.2 us (14%)
  other arithmetic  14.4 us (8%)
  starting transfers between devices  7.61 us (4%)
    ppermute x3, waiting for transfers between devices, shifted(): return lax.ppermute(value, axis, pairs)  46.3 us
    dot_general x168, matrix products, matmul(): jnp.matmul(left, right, precision=PRECISE, preferred_element_type=jnp.flo...  44.7 us
    psum x1, blocking collectives, local(): off_total, diag_total = lax.psum((off_local, diag_local), 'blk')  18 us
    all_gather x3, blocking collectives, local(): lax.all_gather(work_x, axis_name=axis_name)  17.6 us
    ppermute x3, starting transfers between devices, shifted(): return lax.ppermute(value, axis, pairs)  7.61 us
    reduce_max x9, other arithmetic, orthonormal(): bound = jnp.max(jnp.sum(jnp.abs(inner), axis=1))  5.47 us
    div x1, other arithmetic, local(): return (current, jnp.sqrt(off_sums) / jnp.sqrt(diag_sums))  4.33 us
  transfers between devices with their start and end apart: 3, of which 3 were waited for; matrix products, arithmetic and copies ran while one was open for 0% of the time, Pallas kernels for 0%

profile of v1, /device:TPU:0, one launch (start us, length us, event | category | flops | bytes accessed | tf_op | source)
XLA Modules:
  0.0 175.5 jit_solution(11053742610367515310)
XLA Ops:
  0.6 1.6 fusion.124
  19.2 1.0 fusion.125
  20.2 6.5 %all-gather = f32[256,64]{1,0:T(8,128)S(1)} all-gather(f32[64,64]{1,0:T(8,128)S(1)} %fusion.125), channel_id=2, replica_groups=mesh['blk'=8,'rows'=4] {'rows'}, dimensions={0}, use_global_device_ids=true | all-gather | bytes 81920 | tf_op jit(solution)/shard_map/all_gather | solution.py:55
  26.7 0.7 multiply_reduce_fusion.2
  42.7 1.0 fusion.147
  43.8 15.7 %conditional.3 = (f32[32,4096]{1,0:T(8,128)}) conditional(s32[]{:T(128)} %clamp.9, f32[32,4096]{1,0:T(8,128)S(1)} %get-tuple-element.64, f32[32,4096]{1,0:T(8,128)S(1)} %get-tuple-element.64, f32[32,4096]{1,0:T(8,128)S(1)} %get-tuple-element.64, f32[32,4096]{1,0:T(8,128)S(1)} %get-tuple-element.64, ...), branch_computations={%region_10.11_spmd, %region_11.12_spmd, %region_12.13_spmd, %regio... | conditional | bytes 2097200 | solution.py:74
  43.8 4.0 %collective-permute-start.5 = (f32[32,4096]{1,0:T(8,128)S(1)}, f32[32,4096]{1,0:T(8,128)}, u32[]{:S(2)}, u32[]{:S(2)}) collective-permute-start(f32[32,4096]{1,0:T(8,128)S(1)} %param.5), channel_id=1, source_target_pairs={{0,24},{4,28},{8,0},{12,4},{16,8},{20,12},{24,16},{28,20},{1,25},{... | collective-permute-start | bytes 1572872 | tf_op jit(solution)/shard_map/cond/branch_5_fun/ppermute | solution.py:16
  47.8 11.7 %collective-permute-done.5 = f32[32,4096]{1,0:T(8,128)} collective-permute-done((f32[32,4096]{1,0:T(8,128)S(1)}, f32[32,4096]{1,0:T(8,128)}, u32[]{:S(2)}, u32[]{:S(2)}) %collective-permute-start.5) | collective-permute-done | bytes 524320 | tf_op jit(solution)/shard_map/cond/branch_5_fun/ppermute | solution.py:16
  59.5 2.7 %fusion.84 = f32[64,64]{1,0:T(8,128)S(1)} fusion(f32[32,4096]{1,0:T(8,128)} %get-tuple-element.89, f32[32,4096]{1,0:T(8,128)S(1)} %get-tuple-element.63, pred[]{:T(512)S(6)} %ne.49), kind=kOutput, calls=%fused_computation.168 | convolution fusion | flops 202113024 | bytes 1064961 | tf_op jit(solution)/shard_map/dot_general | solution.py:20
  62.3 5.6 %all-gather.1 = f32[256,64]{1,0:T(8,128)S(1)} all-gather(f32[64,64]{1,0:T(8,128)S(1)} %fusion.84), channel_id=3, replica_groups=mesh['blk'=8,'rows'=4] {'rows'}, dimensions={0}, use_global_device_ids=true | all-gather | bytes 81920 | tf_op jit(solution)/shard_map/all_gather | solution.py:55
  67.9 0.7 multiply_reduce_fusion.1
  83.8 2.3 %fusion.83 = f32[64,4096]{1,0:T(8,128)S(1)} fusion(f32[64,64]{1,0:T(8,128)S(1)} %fusion.24, f32[32,4096]{1,0:T(8,128)} %get-tuple-element.89, f32[32,4096]{1,0:T(8,128)S(1)} %get-tuple-element.63, pred[]{:T(512)S(6)} %ne.49), kind=kOutput, calls=%fused_computation.167 | convolution fusion | flops 202113024 | bytes 2113537 | tf_op jit(solution)/shard_map/dot_general | solution.py:20
  86.2 27.4 %conditional.4 = (f32[32,4096]{1,0:T(8,128)}) conditional(s32[]{:T(128)} %clamp.10, f32[32,4096]{1,0:T(8,128)S(1)} %get-tuple-element.62, f32[32,4096]{1,0:T(8,128)S(1)} %get-tuple-element.62, f32[32,4096]{1,0:T(8,128)S(1)} %get-tuple-element.62, f32[32,4096]{1,0:T(8,128)S(1)} %get-tuple-element.62, ...), branch_computations={%region_27.28_spmd, %region_28.29_spmd, %region_29.30_spmd, %regio... | conditional | bytes 2097200 | solution.py:74
  86.2 1.5 collective-permute-start.9
  87.8 25.8 %collective-permute-done.9 = f32[32,4096]{1,0:T(8,128)} collective-permute-done((f32[32,4096]{1,0:T(8,128)S(1)}, f32[32,4096]{1,0:T(8,128)}, u32[]{:S(2)}, u32[]{:S(2)}) %collective-permute-start.9) | collective-permute-done | bytes 524320 | tf_op jit(solution)/shard_map/cond/branch_2_fun/ppermute | solution.py:16
  113.6 2.7 %fusion.82 = f32[64,64]{1,0:T(8,128)S(1)} fusion(f32[32,4096]{1,0:T(8,128)} %get-tuple-element.90, f32[32,4096]{1,0:T(8,128)S(1)} %get-tuple-element.61, pred[]{:T(512)S(6)} %ne.48), kind=kOutput, calls=%fused_computation.166 | convolution fusion | flops 202113024 | bytes 1064961 | tf_op jit(solution)/shard_map/dot_general | solution.py:20
  116.3 5.4 %all-gather.2 = f32[256,64]{1,0:T(8,128)S(1)} all-gather(f32[64,64]{1,0:T(8,128)S(1)} %fusion.82), channel_id=4, replica_groups=mesh['blk'=8,'rows'=4] {'rows'}, dimensions={0}, use_global_device_ids=true | all-gather | bytes 81920 | tf_op jit(solution)/shard_map/all_gather | solution.py:55
  122.3 18.0 %all-reduce = (f32[1]{0:T(128)}, f32[1]{0:T(128)}, f32[1]{0:T(128)}, f32[1]{0:T(128)}, f32[1]{0:T(128)}, /*index=5*/f32[1]{0:T(128)}) all-reduce(f32[1]{0:T(128)} %bitcast.11, f32[1]{0:T(128)} %bitcast.10, f32[1]{0:T(128)} %bitcast.9, f32[1]{0:T(128)} %bitcast.14, f32[1]{0:T(128)} %bitcast.13, ...), channel_id=1, replica_groups=mesh['blk'=8,'rows'=4] {'blk'}, use_global_device_ids=true, to_apply=%region_56.57 | all-reduce | flops 6 | bytes 48 | tf_op jit(solution)/shard_map/psum | solution.py:62
  140.4 4.3 %fusion.119 = f32[3]{0:T(128)} fusion(f32[1]{0:T(128)} %get-tuple-element.53, f32[1]{0:T(128)} %get-tuple-element.54, f32[1]{0:T(128)} %get-tuple-element.55, f32[1]{0:T(128)} %get-tuple-element.56, f32[1]{0:T(128)} %get-tuple-element.57, f32[1]{0:T(128)} %get-tuple-element.58), kind=kLoop, calls=%fused_computation.235 | loop fusion | flops 15 | bytes 36 | tf_op jit(solution)/shard_map/div | solution.py:82
  160.0 2.3 %fusion.81 = f32[64,4096]{1,0:T(8,128)S(1)} fusion(f32[64,64]{1,0:T(8,128)S(1)} %fusion, f32[32,4096]{1,0:T(8,128)} %get-tuple-element.90, f32[32,4096]{1,0:T(8,128)S(1)} %get-tuple-element.61, pred[]{:T(512)S(6)} %ne.48), kind=kOutput, calls=%fused_computation.165 | convolution fusion | flops 202113024 | bytes 2113537 | tf_op jit(solution)/shard_map/dot_general | solution.py:20
  162.3 10.9 %conditional.5 = (f32[32,4096]{1,0:T(8,128)}) conditional(s32[]{:T(128)} %clamp.11, f32[32,4096]{1,0:T(8,128)S(1)} %get-tuple-element.60, f32[32,4096]{1,0:T(8,128)S(1)} %get-tuple-element.60, f32[32,4096]{1,0:T(8,128)S(1)} %get-tuple-element.60, f32[32,4096]{1,0:T(8,128)S(1)} %get-tuple-element.60, ...), branch_computations={%region_44.45_spmd, %region_45.46_spmd, %region_46.47_spmd, %regio... | conditional | bytes 2097200 | solution.py:74
  162.4 2.1 %collective-permute-start.20 = (f32[32,4096]{1,0:T(8,128)S(1)}, f32[32,4096]{1,0:T(8,128)}, u32[]{:S(2)}, u32[]{:S(2)}) collective-permute-start(f32[32,4096]{1,0:T(8,128)S(1)} %param.20), channel_id=1, source_target_pairs={{0,28},{4,0},{8,4},{12,8},{16,12},{20,16},{24,20},{28,24},{1,29},{... | collective-permute-start | bytes 1572872 | tf_op jit(solution)/shard_map/cond/branch_6_fun/ppermute | solution.py:16
  164.4 8.8 %collective-permute-done.20 = f32[32,4096]{1,0:T(8,128)} collective-permute-done((f32[32,4096]{1,0:T(8,128)S(1)}, f32[32,4096]{1,0:T(8,128)}, u32[]{:S(2)}, u32[]{:S(2)}) %collective-permute-start.20) | collective-permute-done | bytes 524320 | tf_op jit(solution)/shard_map/cond/branch_6_fun/ppermute | solution.py:16
  173.2 2.3 %maximum_select_fusion.2 = f32[64,4096]{1,0:T(8,128)} fusion(f32[32,4096]{1,0:T(8,128)} %get-tuple-element.91, f32[32,4096]{1,0:T(8,128)S(1)} %get-tuple-element.59, pred[]{:T(512)S(6)} %ne.47), kind=kLoop, calls=%fused_computation.164 | loop fusion | flops 786432 | bytes 2097153 | tf_op jit(solution)/shard_map/jit(_where)/select_n | solution.py:75
  (198 shorter events, 39.2 us)
Async XLA Ops:
  0.6 18.6 %copy-start = (f32[64,4096]{1,0:T(8,128)S(1)}, f32[64,4096]{1,0:T(8,128)}, u32[]{:S(2)}) copy-start(f32[64,4096]{1,0:T(8,128)} %param.23) | copy-start | bytes 3145732
  43.8 15.7 %collective-permute-start.5 = (f32[32,4096]{1,0:T(8,128)S(1)}, f32[32,4096]{1,0:T(8,128)}, u32[]{:S(2)}, u32[]{:S(2)}) collective-permute-start(f32[32,4096]{1,0:T(8,128)S(1)} %param.5), channel_id=1, source_target_pairs={{0,24},{4,28},{8,0},{12,4},{16,8},{20,12},{24,16},{28,20},{1,25},{... | collective-permute-start | bytes 1572872 | tf_op jit(solution)/shard_map/cond/branch_5_fun/ppermute | solution.py:16
  86.2 27.4 %collective-permute-start.9 = (f32[32,4096]{1,0:T(8,128)S(1)}, f32[32,4096]{1,0:T(8,128)}, u32[]{:S(2)}, u32[]{:S(2)}) collective-permute-start(f32[32,4096]{1,0:T(8,128)S(1)} %param.9), channel_id=1, source_target_pairs={{0,12},{4,16},{8,20},{12,24},{16,28},{20,0},{24,4},{28,8},{1,13},{... | collective-permute-start | bytes 1572872 | tf_op jit(solution)/shard_map/cond/branch_2_fun/ppermute | solution.py:16
  162.4 10.9 %collective-permute-start.20 = (f32[32,4096]{1,0:T(8,128)S(1)}, f32[32,4096]{1,0:T(8,128)}, u32[]{:S(2)}, u32[]{:S(2)}) collective-permute-start(f32[32,4096]{1,0:T(8,128)S(1)} %param.20), channel_id=1, source_target_pairs={{0,28},{4,0},{8,4},{12,8},{16,12},{20,16},{24,20},{28,24},{1,29},{... | collective-permute-start | bytes 1572872 | tf_op jit(solution)/shard_map/cond/branch_6_fun/ppermute | solution.py:16
